TPU v7x, 256 devices: a whole 4x4x8 slice. The times are simulated.
256 devices in a mesh: cells: 64 (over x, z_lo, y), genes: 4 (over z_hi, core).
Axes of the slice: x: 4, y: 4, z: 8 (z_hi: 2, z_lo: 4; z = z_hi * 4 + z_lo), core: 2. Of those that a mesh axis runs over, the one named last changes fastest.
Arguments:
- counts: int32 [65536, 4096], P('cells', 'genes'), may hold values from 0 to 26, as said below
- library: int32 [65536], P('cells'), may hold values from 2000 to 19999
Outputs:
- adjacency: float32 [4096, 4096], P('cells', 'genes')
- connectivity: float32 [4096], P('cells')
Inputs may be any that keep to these rules, and one draw needn't show every extreme that they name: Non-negative integer counts.
All inputs are finite; a program needn't handle non-finite values.
Results may differ from a plain program's by a relative error of at most 0.006.
Values may be sent and summed in bfloat16 or wider, within the bound.
A program may use at most 128 MiB of HBM per device.

v0:
```python
import jax
import jax.numpy as jnp
from jax import lax
from jax.sharding import Mesh
from jax.sharding import PartitionSpec as P

CELLS = ("cells_0", "cells_1", "cells_2")


def from_everyone(x, axis):
    copies = jnp.broadcast_to(x, (lax.axis_size(axis), *x.shape))
    return lax.all_to_all(copies, axis, split_axis=0, concat_axis=0, tiled=True)


def of_everyone(x, axis):
    return from_everyone(x, axis).sum(axis=0)


def packed_total(arrays, axis):
    ends = [0]
    for a in arrays:
        ends.append(ends[-1] + a.size)
    total = of_everyone(jnp.concatenate([a.ravel() for a in arrays]), axis)
    return tuple((total[b:e].reshape(a.shape) for a, b, e in zip(arrays, ends, ends[1:])))


def turned_gather(arrays, axis, dims):
    turned = [jnp.moveaxis(a, dim, 0) for a, dim in zip(arrays, dims)]
    both = jnp.concatenate([t.reshape(len(t), -1) for t in turned], axis=1)
    out, at, outs = (lax.all_gather(both, axis, axis=0, tiled=True), 0, [])
    for t, dim in zip(turned, dims):
        section = out[:, at : at + t[0].size].reshape(-1, *t.shape[1:])
        outs.append(jnp.moveaxis(section, 0, dim))
        at += t[0].size
    return tuple(outs)


def sum_in_order(blocks, axes, sequence):
    inside = blocks.shape[1:]
    blocks = blocks.reshape(*(lax.axis_size(a) for a in axes), *inside)
    blocks = jnp.moveaxis(blocks, sequence, range(len(axes))).reshape(-1, *inside)
    for k in sequence:
        blocks = lax.psum_scatter(blocks, axes[k], scatter_dimension=0, tiled=True)
    return blocks[0]


def cut_along(x, dim, devices):
    dims = x.shape
    blocks = x.reshape(*dims[:dim], devices, dims[dim] // devices, *dims[dim + 1 :])
    return jnp.moveaxis(blocks, dim, 0)


def scatter_axes(x, axes, sequence, dim):
    devices = lax.axis_size(axes)
    return sum_in_order(cut_along(x, dim, devices), axes, sequence)


def normalize(counts, library):
    factor = 10000.0 / library.astype(jnp.float32)
    return jnp.log1p(counts.astype(jnp.float32) * factor[:, None]).astype(jnp.bfloat16)


def cross_product(left, right):
    return lax.dot_general(
        left, right, (((0,), (0,)), ((), ())), preferred_element_type=jnp.float32
    )


def shards(counts, library):
    own_block = normalize(counts, library)
    col_width = own_block.shape[1]
    cell_groups = lax.axis_size(CELLS)
    gene_total = col_width * lax.axis_size("genes")
    row_width = gene_total // cell_groups
    total_cells = float(counts.shape[0] * cell_groups)
    widened = own_block.astype(jnp.float32)
    local_sums = jnp.sum(widened, axis=0)
    local_squares = jnp.sum(widened * widened, axis=0)
    block_sums, block_squares = packed_total((local_sums, local_squares), CELLS)
    gene_sums, gene_squares = turned_gather((block_sums, block_squares), "genes", (0, 0))
    full_block = lax.all_gather(own_block, "genes", axis=1, tiled=True)
    gram_tile = scatter_axes(cross_product(full_block, own_block), CELLS, (0, 2, 1), 0)
    means = gene_sums / total_cells
    variances = gene_squares / total_cells - means * means
    scales = lax.rsqrt(variances + 1e-05)
    row_first = lax.axis_index(CELLS) * row_width
    col_first = lax.axis_index("genes") * col_width
    row_means = lax.dynamic_slice_in_dim(means, row_first, row_width, 0)
    col_means = lax.dynamic_slice_in_dim(means, col_first, col_width, 0)
    row_scales = lax.dynamic_slice_in_dim(scales, row_first, row_width, 0)
    col_scales = lax.dynamic_slice_in_dim(scales, col_first, col_width, 0)
    correlation = (
        (gram_tile / total_cells - row_means[:, None] * col_means[None, :])
        * row_scales[:, None]
        * col_scales[None, :]
    )
    powered = correlation**6
    row_index = row_first + jnp.arange(row_width, dtype=jnp.int32)[:, None]
    col_index = col_first + jnp.arange(col_width, dtype=jnp.int32)[None, :]
    adjacency = jnp.where(row_index == col_index, jnp.float32(0.0), powered)
    connectivity = of_everyone(jnp.sum(adjacency, axis=1), "genes")
    return (adjacency, connectivity)


def solution(mesh):
    finer = Mesh(
        mesh.devices.reshape(4, 4, 4, mesh.shape["genes"]),
        ("cells_0", "cells_1", "cells_2", "genes"),
    )
    in_specs = (P(CELLS, "genes"), P(CELLS))
    out_specs = (P(CELLS, "genes"), P(CELLS))
    return jax.shard_map(
        shards, mesh=finer, in_specs=in_specs, out_specs=out_specs, check_vma=False
    )
```

profile of v0, /device:TPU:1, one launch (start us, length us, event | category | flops | bytes accessed | tf_op | source)
XLA Modules:
  0.0 405.9 jit_solution(15591229205354031744)
XLA Ops:
  7.2 0.0 all-gather.2.cloned.1.call-start
  7.2 0.7 convert_divide_fusion
  7.9 5.6 %convert_reduce_fusion = (f32[1024]{0:T(1024)S(1)}, f32[1024]{0:T(1024)S(1)}, bf16[1024,1024]{1,0:T(8,128)(2,1)}) fusion(f32[1024]{0:T(1024)S(1)} %convert_divide_fusion, s32[1024,1024]{1,0:T(8,128)} %param.2), kind=kLoop, calls=%fused_computation.1 | loop fusion | flops 7337984 | bytes 6303744 | tf_op jit(solution)/shard_map/reduce_sum | solution.py:77
  13.5 0.0 all-gather.2.cloned.1.call-update
  13.6 0.0 reduce-scatter.4.cloned.1.call-start
  13.6 117.8 %all-gather.2.cloned.1.call-done = bf16[1024,4096]{1,0:T(8,128)(2,1)} async-done(((bf16[1024,1024]{1,0:T(8,128)(2,1)}), bf16[1024,4096]{1,0:T(8,128)(2,1)}) %all-gather.2.cloned.1.call-update) | async-done | bytes 8388624 | tf_op jit(solution)/shard_map/all_gather | solution.py:81
  131.4 12.0 %fusion.11 = f32[4096,1024]{1,0:T(8,128)S(1)} fusion(bf16[1024,4096]{1,0:T(8,128)(2,1)} %all-gather.2.cloned.1.call-done, bf16[1024,1024]{1,0:T(8,128)(2,1)} %get-tuple-element.6), kind=kOutput, calls=%fused_computation.27 | convolution fusion | flops 8589934592 | bytes 27262976 | tf_op jit(solution)/shard_map/dot_general | solution.py:64
  143.5 6.6 %copy.6 = f32[4,4,4,64,1024]{4,3,2,1,0:T(8,128)} copy(f32[4,4,4,64,1024]{4,3,1,2,0:T(8,128)S(1)} %bitcast.27) | data formatting | bytes 33554432 | tf_op jit(solution)/shard_map/transpose | solution.py:41
  150.0 0.0 reduce-scatter.4.cloned.1.call-update
  150.1 0.0 reduce-scatter.6.cloned.1.call-start
  150.1 146.2 %reduce-scatter.4.cloned.1.call-done = f32[16,64,1024]{2,1,0:T(8,128)} async-done(((f32[64,64,1024]{2,1,0:T(8,128)}), f32[16,64,1024]{2,1,0:T(8,128)}) %reduce-scatter.4.cloned.1.call-update) | async-done | bytes 4194320 | tf_op jit(solution)/shard_map/reduce_scatter | solution.py:43
  296.3 0.0 reduce-scatter.6.cloned.1.call-update
  296.4 1.1 broadcast_in_dim.8
  297.4 8.9 %all-to-all-start = ((f32[64,1,2048]{2,1,0:T(1,128)}), f32[64,1,2048]{2,1,0:T(1,128)S(1)}, u32[]{:S(2)}, u32[]{:S(2)}) async-start(f32[64,1,2048]{2,1,0:T(1,128)} %broadcast_in_dim.8), calls=%async_computation.3 | async-start | bytes 1048576 | tf_op jit(solution)/shard_map/all_to_all | solution.py:12
  306.3 0.0 reduce-scatter.8.cloned.1.call-start
  306.4 45.9 %reduce-scatter.6.cloned.1.call-done = f32[4,64,1024]{2,1,0:T(8,128)} async-done(((f32[16,64,1024]{2,1,0:T(8,128)}), f32[4,64,1024]{2,1,0:T(8,128)}) %reduce-scatter.6.cloned.1.call-update) | async-done | bytes 1048592 | tf_op jit(solution)/shard_map/reduce_scatter | solution.py:43
  352.3 0.0 reduce-scatter.8.cloned.1.call-update
  352.3 0.3 reduce_sum.47
  352.7 9.6 %all_gather.7 = f32[4096,2]{0,1:T(2,128)S(1)} all-gather(f32[1024,2]{0,1:T(2,128)S(1)} %pad_maximum_fusion.1), channel_id=1, replica_groups=mesh['cells_0'=4,'cells_1'=4,'cells_2'=4,'genes'=4] {'genes'}, dimensions={0}, use_global_device_ids=true | all-gather | bytes 40960 | tf_op jit(solution)/shard_map/all_gather | solution.py:30
  362.3 0.1 fusion.6
  362.4 22.1 %reduce-scatter.8.cloned.1.call-done = f32[1,64,1024]{2,1,0:T(8,128)} async-done(((f32[4,64,1024]{2,1,0:T(8,128)}), f32[1,64,1024]{2,1,0:T(8,128)}) %reduce-scatter.8.cloned.1.call-update) | async-done | bytes 262160 | tf_op jit(solution)/shard_map/reduce_scatter | solution.py:43
  384.4 1.9 fusion.8
  386.4 12.4 %all_to_all.12 = f32[4,1,64]{2,1,0:T(1,128)S(1)} all-to-all(f32[4,1,64]{2,1,0:T(1,128)S(1)} %broadcast_in_dim.10), channel_id=1, replica_groups=mesh['cells_0'=4,'cells_1'=4,'cells_2'=4,'genes'=4] {'genes'}, dimensions={0} | all-to-all | bytes 2048 | tf_op jit(solution)/shard_map/all_to_all | solution.py:12
  398.8 0.5 reduce_sum.49
  (9 shorter events, 0.1 us)
Async XLA Ops:
  7.2 124.3 %all-gather.2.cloned.1.call-start = ((), (), s32[]{:S(2)}) async-start(), calls=%async_computation.5 | async-start | bytes 10485760 | tf_op jit(solution)/shard_map/all_gather | solution.py:81
  13.6 282.8 %reduce-scatter.4.cloned.1.call-start = ((), (), s32[]{:S(2)}) async-start(), calls=%async_computation.6 | async-start | bytes 20971520 | tf_op jit(solution)/shard_map/reduce_scatter | solution.py:43
  150.1 202.2 %reduce-scatter.6.cloned.1.call-start = ((), (), s32[]{:S(2)}) async-start(), calls=%async_computation.7 | async-start | bytes 5242880 | tf_op jit(solution)/shard_map/reduce_scatter | solution.py:43
  297.4 54.9 %all-to-all-start = ((f32[64,1,2048]{2,1,0:T(1,128)}), f32[64,1,2048]{2,1,0:T(1,128)S(1)}, u32[]{:S(2)}, u32[]{:S(2)}) async-start(f32[64,1,2048]{2,1,0:T(1,128)} %broadcast_in_dim.8), calls=%async_computation.3 | async-start | bytes 1048576 | tf_op jit(solution)/shard_map/all_to_all | solution.py:12
  306.3 78.1 %reduce-scatter.8.cloned.1.call-start = ((), (), s32[]{:S(2)}) async-start(), calls=%async_computation.8 | async-start | bytes 1310720 | tf_op jit(solution)/shard_map/reduce_scatter | solution.py:43
Sparse Core Ops, SparseCore 0:
  13.7 117.6 all-gather.1
  150.2 146.0 reduce-scatter.3
  298.9 53.3 reduce-scatter.5
  354.7 29.7 reduce-scatter.7
where the time goes:
time: 406 us
  waiting for transfers between devices  332 us (82%)
  blocking collectives  22 us (5%)
  between operations  13.8 us (3%)
  matrix products  12 us (3%)
  other arithmetic  9.16 us (2%)
  starting transfers between devices  9.05 us (2%)
  local copies, waits for them, and re-layouts  7.75 us (2%)
    reduce_scatter x3, waiting for transfers between devices, sum_in_order(): blocks = lax.psum_scatter(blocks, axes[k], scatter_dimension=0, tiled=True)  214 us
    all_gather x1, waiting for transfers between devices, shards(): full_block = lax.all_gather(own_block, 'genes', axis=1, tiled=True)  118 us
    all_to_all x1, blocking collectives, from_everyone(): return lax.all_to_all(copies, axis, split_axis=0, concat_axis=0, tiled=True)  12.4 us
    dot_general x1, matrix products, cross_product(): lax.dot_general(left, right, (((0,), (0,)), ((), ())), preferred_element_...  12 us
    all_gather x1, blocking collectives, turned_gather(): out, at, outs = (lax.all_gather(both, axis, axis=0, tiled=True), 0, [])  9.55 us
    all_to_all x1, starting transfers between devices, from_everyone(): return lax.all_to_all(copies, axis, split_axis=0, concat_axis=0, tiled=True)  8.89 us
  transfers between devices with their start and end apart: 5, of which 4 were waited for; matrix products, arithmetic and copies ran while one was open for 0% of the time, Pallas kernels for 0%

commit v1 on v0

v1 whole, which is shorter than its diff:
```python
import functools

import jax
import jax.numpy as jnp
from jax import lax
from jax.experimental import pallas as pl
from jax.experimental.pallas import tpu as pltpu
from jax.sharding import Mesh
from jax.sharding import PartitionSpec as P

MESH = pl.DeviceIdType.MESH
BLOCK = 1024
SUB = 64
QUARTER = 256
LEVELS = 8190.0
CELLS_ALL = 65536.0


def kernel(
    x_ref, stat_ref, adj_ref, conn_ref,
    xa, xb, rl, tt, f1, d1, r1, f2, d2, r2, zs, zr, ms, mr,
    sz, sx, sy, sc, sq, cm, cu, cw, rowv, cr, csend,
    load_sem, send_sem, recv_sem,
):
    x, zl, y = lax.axis_index("x"), lax.axis_index("zl"), lax.axis_index("y")
    zh, k = lax.axis_index("zh"), lax.axis_index("k")
    z = zh * 4 + zl
    spot = {"x": x, "y": y}
    used = [0]
    started = []

    def remote(src, dst, where, slot=None):
        n = used[0]
        used[0] += 1
        copy = pltpu.make_async_remote_copy(
            src_ref=src,
            dst_ref=dst,
            send_sem=send_sem.at[n],
            recv_sem=recv_sem.at[n if slot is None else slot],
            device_id=where,
            device_id_type=MESH,
        )
        copy.start()
        started.append(copy)
        return copy

    def along_z(hops):
        there = lax.rem(z + hops + 8, 8)
        return {"zh": there // 4, "zl": lax.rem(there, 4)}

    def hop(axis, by):
        return {axis: lax.rem(spot[axis] + by + 4, 4)}

    load = pltpu.make_async_copy(x_ref, xa.at[k], load_sem)
    load.start()
    sz[z] = stat_ref[...]
    stat_z = [remote(stat_ref, sz.at[z], along_z(d)) for d in range(1, 8)]
    load.wait()

    far_half = (1 - zh) * 512

    def leg_one(i):
        return [
            remote(
                xa.at[k, i, pl.ds(far_half + 256 * f, 256)],
                rl.at[f, i],
                along_z(2 - 4 * f),
            )
            for f in range(2)
        ]

    def leg_two(i):
        for c in first_legs[i]:
            c.wait_recv()
        second_legs[i] = [
            remote(rl.at[f, i], xb.at[k, i, pl.ds(256 * f, 256)], along_z(2 - 4 * f))
            for f in range(2)
        ]

    def to_partner(i):
        for c in second_legs[i]:
            c.wait_recv()
        return remote(xb.at[k, i], xb.at[k, i], {"k": 1 - k})

    first_legs, second_legs, partner_b = {}, {}, {}
    first_legs[0], first_legs[1] = leg_one(0), leg_one(1)
    partner_x = remote(xa.at[k], xa.at[k], {"k": 1 - k})

    for c in stat_z:
        c.wait_recv()
    def column(h):
        parts = [(sz[4 * h + i, b : b + 1], sz[4 * h + i, 2 + b : 3 + b]) for i in range(4) for b in range(2)]
        total = functools.reduce(jnp.add, [p[0] for p in parts])
        squares = functools.reduce(jnp.add, [p[1] for p in parts])
        mean = total * (1.0 / 4096.0)
        norms = [p[1] - 2.0 * mean * p[0] + 512.0 * mean * mean for p in parts]
        norm = functools.reduce(jnp.maximum, norms) * 1.0001 + squares * 2.5e-7 + 1e-2
        return total, squares, jnp.sqrt(norm)

    for h in range(2):
        for i, v in enumerate(column(h)):
            sx[x, 4 * h + i : 4 * h + i + 1] = v

    def spread(ref, axis, cells, out, slot):
        here = spot[axis]
        copies = [remote(ref.at[here], ref.at[here], hop(axis, d)) for d in (1, 3, 2)]
        for c in copies:
            c.wait_recv()
        for h in range(2):
            parts = [[ref[i, 4 * h + r : 4 * h + r + 1] for r in range(3)] for i in range(4)]
            total = parts[0][0] + parts[1][0] + parts[2][0] + parts[3][0]
            squares = parts[0][1] + parts[1][1] + parts[2][1] + parts[3][1]
            mean = total * (0.25 / cells)
            norms = [p[2] + (512.0**0.5) * jnp.abs(p[0] * (1.0 / cells) - mean) for p in parts]
            norm = functools.reduce(jnp.maximum, norms)
            for i, v in enumerate((total, squares, norm)):
                out[slot, 4 * h + i : 4 * h + i + 1] = v

    spread(sx, "x", 4096.0, sy, y)
    spread(sy, "y", 16384.0, sc, k)
    other_core = remote(sc.at[k], sc.at[k], {"k": 1 - k})
    leg_two(0)
    other_core.wait_recv()
    for b in range(4):
        h, core = b // 2, b % 2
        rows = sc[core, 4 * h : 4 * h + 4]
        mean = rows[0:1] * (1.0 / CELLS_ALL)
        unit = (LEVELS / 2.0) ** 0.5 / rows[2:3]
        variance = rows[1:2] * (1.0 / CELLS_ALL) - mean * mean
        weight = lax.rsqrt(variance + 1e-05) / unit
        rowv[b, 0:1] = mean
        rowv[b, 1:2] = unit
        rowv[b, 2:3] = weight
        cm[b] = jnp.broadcast_to(mean, (128, BLOCK)).T
        cu[b] = jnp.broadcast_to(unit, (128, BLOCK)).T
    cw[...] = jnp.broadcast_to(rowv[x, 2:3], (128, BLOCK)).T
    mine = 2 * zh + k
    own_mean, own_unit = rowv[mine, 0:1], rowv[mine, 1:2]
    scaled_mean = own_mean * own_unit
    half_sum = stat_ref[pl.ds(zh, 1)]
    for e, total in enumerate((stat_ref[0:1] + stat_ref[1:2], half_sum)):
        sq[e, 0:1] = scaled_mean * (1.0 + e)
        sq[e, 1:2] = total * own_unit * (1.0 + e)
    sq[0, 2:3] = own_unit
    sq[1, 2:3] = own_unit * 2.0

    def products(e, lo):
        depth = 512 if e else 1024
        side = lax.rem(zh + e, 2)
        ones = jnp.ones((depth, 128), jnp.bfloat16)

        def body(t, carry):
            a, hi = t // 2, lax.rem(t, 2)
            left = (xb if e else xa)[a, 2 * lo + hi]
            turned = left.T
            first = pl.multiple_of((2 * hi + lo) * QUARTER, QUARTER)
            mean = cm[2 * side + a, pl.ds(first, QUARTER)]
            unit = cu[2 * side + a, pl.ds(first, QUARTER)]
            total = jnp.dot(turned, ones, preferred_element_type=jnp.float32)
            off = (total - float(depth) * mean) * unit
            mean = mean * unit
            wide = lambda v: jnp.concatenate([v, v], axis=1)
            unit, off, mean = wide(unit), wide(off), wide(mean)
            for q in range(4):
                g = (q % 2) * 2 + q // 2
                if e:
                    right = xa[k, g, pl.ds(pl.multiple_of(zh * 512, 512), 512)]
                else:
                    right = xa[k, g]
                gram = jnp.dot(turned, right, preferred_element_type=jnp.float32)
                at = pl.ds(q * QUARTER, QUARTER)
                value = (
                    gram * unit * sq[e, 2:3, at]
                    - off * sq[e, 0:1, at]
                    - mean * sq[e, 1:2, at]
                )
                value = jnp.clip(value, -LEVELS, LEVELS)
                code = jnp.round(value).astype(jnp.int32).astype(jnp.int16)
                code = code.reshape(4, SUB, QUARTER)
                if q < 2:
                    tt[2 * e + lo, q, t] = code
                else:
                    tt[2 * e + lo, q, :, pl.ds(t, 1)] = code[:, None]
            return carry

        lax.fori_loop(0, 4, body, 0)

    axes = [("x", "y", -1), ("x", "y", 1), ("y", "x", -1), ("y", "x", 1)]

    def at4(axis, by):
        return lax.rem(spot[axis] + by + 4, 4)

    class Ring:
        def __init__(self, tile, axis, s, far, direct, relay):
            self.tile, self.axis, self.s = tile, axis, s
            self.far, self.direct, self.relay = far, direct, relay

        def start(self):
            s = self.s
            self.c_far = remote(
                self.tile(at4(self.axis, 2)), self.far, hop(self.axis, s)
            )
            self.c_direct = remote(
                self.tile(at4(self.axis, -s)), self.direct, hop(self.axis, -s)
            )

        def pass_on(self):
            s = self.s
            self.c_far.wait_recv()
            here = self.tile(at4(self.axis, s))
            here[...] = here[...] + self.far[...]
            self.c_relay = remote(here, self.relay, hop(self.axis, s))

        def total(self):
            self.c_direct.wait_recv()
            self.c_relay.wait_recv()
            here = self.tile(spot[self.axis])
            return here[...] + self.direct[...] + self.relay[...]

    rings1, rings2 = {}, {}

    def p1(j):
        for q, (first, _, s) in enumerate(axes):
            ring = Ring(
                lambda d, q=q: tt.at[j, q, d],
                first, s, f1.at[j, q], d1.at[j, q], r1.at[j, q],
            )
            rings1[j, q] = ring
            ring.start()

    def p2(j):
        for q in range(4):
            rings1[j, q].pass_on()

    def p3(j):
        for q, (first, second, s) in enumerate(axes):
            total = rings1[j, q].total().astype(jnp.int32)
            here = spot[first]
            tt[j, q, here] = ((total + 2) >> 2).astype(jnp.int16)
            ring = Ring(
                lambda d, q=q, here=here: tt.at[j, q, here, d],
                second, s, f2.at[j, q], d2.at[j, q], r2.at[j, q],
            )
            rings2[j, q] = ring
            ring.start()

    def p4(j):
        for q in range(4):
            rings2[j, q].pass_on()

    def p5(j):
        e, lo = j // 2, j % 2
        for q in range(4):
            zs[j, :, q * QUARTER : (q + 1) * QUARTER] = rings2[j, q].total()
        to_x = 2 * lax.rem(zh + e, 2) + x // 2
        to_zl = 2 * lax.rem(x, 2) + lo
        stays = jnp.logical_and(to_x == x, to_zl == zl)
        n = used[0]
        used[0] += 1
        copy = pltpu.make_async_remote_copy(
            src_ref=zs.at[j],
            dst_ref=zr.at[zl],
            send_sem=send_sem.at[n],
            recv_sem=recv_sem.at[LAST + zl],
            device_id={"x": to_x, "zl": to_zl},
            device_id_type=MESH,
        )

        @pl.when(jnp.logical_not(stays))
        def _():
            copy.start()

        @pl.when(stays)
        def _():
            zr[zl] = zs[j]

        last_sends.append((stays, copy))

    last_sends = []

    leg_two(1)
    first_legs[2], first_legs[3] = leg_one(2), leg_one(3)
    partner_x.wait_recv()
    products(0, 0)
    p1(0)
    products(0, 1)
    p1(1)
    p2(0)
    leg_two(2)
    p2(1)
    partner_b[0] = to_partner(0)
    partner_b[1] = to_partner(1)
    p3(0)
    partner_b[0].wait_recv()
    partner_b[1].wait_recv()
    products(1, 0)
    p1(2)
    leg_two(3)
    p3(1)
    p4(0)
    p4(1)
    p2(2)
    p5(0)
    p5(1)
    partner_b[2] = to_partner(2)
    p3(2)
    partner_b[3] = to_partner(3)
    partner_b[2].wait_recv()
    partner_b[3].wait_recv()
    products(1, 1)
    p1(3)
    p4(2)
    p2(3)
    p5(2)
    p3(3)
    p4(3)
    p5(3)

    from_x = 2 * lax.rem(x, 2) + zl // 2
    for s in range(4):
        arrives = jnp.logical_not(jnp.logical_and(from_x == x, zl == s))

        @pl.when(arrives)
        def _(s=s):
            pltpu.make_async_remote_copy(
                src_ref=zs.at[0],
                dst_ref=zr.at[s],
                send_sem=send_sem.at[0],
                recv_sem=recv_sem.at[LAST + s],
                device_id={"x": from_x, "zl": s},
                device_id_type=MESH,
            ).wait_recv()

    value = functools.reduce(lambda a, b: a + b, [zr[s].astype(jnp.int32) for s in range(4)])
    csend[...] = value.astype(jnp.float32)
    crossed = (x // 2) != zh

    mirror = []
    for dz in range(4):
        for dy in range(4):
            there_z, there_y = lax.rem(zl + dz, 4), lax.rem(y + dy, 4)
            n = used[0]
            used[0] += 1
            mirror.append(
                pltpu.make_async_remote_copy(
                    src_ref=ms.at[there_z * 4 + there_y],
                    dst_ref=mr.at[zl * 4 + y],
                    send_sem=send_sem.at[n],
                    recv_sem=recv_sem.at[n],
                    device_id={
                        "x": mine, "zl": there_z, "y": there_y,
                        "zh": x // 2, "k": lax.rem(x, 2),
                    },
                    device_id_type=MESH,
                )
            )

    @pl.when(crossed)
    def _():
        odd = lax.rem(y, 2)
        part = csend[...] * 0.25
        csend[...] = csend[...] * 0.5
        flag = odd.astype(jnp.float32)
        both = jnp.concatenate([part * (1.0 - flag), part * flag], axis=0)
        turned = jnp.round(both.T).astype(jnp.int32).astype(jnp.int16)
        ms[...] = turned.reshape(16, SUB, 128)
        for c in mirror:
            c.start()
        for c in mirror:
            c.wait_recv()
        for m in range(8):
            pair = (mr[2 * m] + mr[2 * m + 1]).astype(jnp.int32)
            at = pl.ds(m * 128, 128)
            csend[:, at] = csend[:, at] + 2.0 * pair.astype(jnp.float32)
        for c in mirror:
            c.wait_send()

    first = pl.multiple_of((zl * 4 + y) * SUB, SUB)
    weight = cw[pl.ds(first, SUB)] * (4.0 / CELLS_ALL)
    row = x * BLOCK + first + lax.broadcasted_iota(jnp.int32, (SUB, 128), 0)
    partial = jnp.zeros((SUB, 128), jnp.float32)
    for m in range(8):
        at = pl.ds(m * 128, 128)
        r = csend[:, at] * weight * rowv[mine, 2:3, at]
        r2_ = r * r
        power = r2_ * r2_ * r2_
        column = mine * BLOCK + m * 128 + lax.broadcasted_iota(jnp.int32, (SUB, 128), 1)
        power = jnp.where(row == column, 0.0, power)
        adj_ref[:, at] = power
        partial = partial + power
    conn_ref[...] = partial
    to = [{"k": 1 - k}, {"zh": 1 - zh}, {"k": 1 - k, "zh": 1 - zh}]
    cr[3] = partial
    ends = [remote(cr.at[3], cr.at[i], where) for i, where in enumerate(to)]
    for c in ends:
        c.wait_recv()
    total = cr[0] + cr[1] + cr[2] + cr[3]
    conn_ref[...] = jnp.broadcast_to(jnp.sum(total, axis=1, keepdims=True), (SUB, 128))
    for c in started:
        c.wait_send()
    for stays, copy in last_sends:

        @pl.when(jnp.logical_not(stays))
        def _(copy=copy):
            copy.wait_send()

    assert used[0] <= LAST, used[0]


LAST = 180


def normalize(counts, library):
    factor = 10000.0 / library.astype(jnp.float32)
    return jnp.log1p(counts.astype(jnp.float32) * factor[:, None]).astype(jnp.bfloat16)


def shards(counts, library):
    own = normalize(counts, library)
    wide = own.astype(jnp.float32).reshape(2, 512, BLOCK)
    halves = jnp.sum(wide, axis=1)
    stats = jnp.concatenate([halves, jnp.sum(wide * wide, axis=1)])
    grouped = own.reshape(BLOCK, 2, 2, QUARTER).transpose(2, 1, 0, 3)
    grouped = grouped.reshape(4, BLOCK, QUARTER)
    i16, f32, bf16 = jnp.int16, jnp.float32, jnp.bfloat16
    vmem = pl.BlockSpec(memory_space=pltpu.VMEM)
    wide_buffer = pltpu.VMEM((4, 4, 4, SUB, QUARTER), i16)
    small_buffer = pltpu.VMEM((4, 4, SUB, QUARTER), i16)
    adjacency, connectivity = pl.pallas_call(
        kernel,
        name="network",
        out_shape=(
            jax.ShapeDtypeStruct((SUB, BLOCK), f32),
            jax.ShapeDtypeStruct((SUB, 128), f32),
        ),
        in_specs=[pl.BlockSpec(memory_space=pl.ANY), vmem],
        out_specs=(vmem, vmem),
        scratch_shapes=[
            pltpu.VMEM((2, 4, BLOCK, QUARTER), bf16),
            pltpu.VMEM((2, 4, 512, QUARTER), bf16),
            pltpu.VMEM((2, 4, QUARTER, QUARTER), bf16),
            pltpu.VMEM((4, 4, 4, 4, SUB, QUARTER), i16),
            wide_buffer, wide_buffer, wide_buffer,
            small_buffer, small_buffer, small_buffer,
            pltpu.VMEM((4, SUB, BLOCK), i16),
            pltpu.VMEM((4, SUB, BLOCK), i16),
            pltpu.VMEM((16, SUB, 128), i16),
            pltpu.VMEM((16, SUB, 128), i16),
            pltpu.VMEM((8, 4, BLOCK), f32),
            pltpu.VMEM((4, 8, BLOCK), f32),
            pltpu.VMEM((4, 8, BLOCK), f32),
            pltpu.VMEM((2, 8, BLOCK), f32),
            pltpu.VMEM((2, 8, BLOCK), f32),
            pltpu.VMEM((4, BLOCK, 128), f32),
            pltpu.VMEM((4, BLOCK, 128), f32),
            pltpu.VMEM((BLOCK, 128), f32),
            pltpu.VMEM((4, 8, BLOCK), f32),
            pltpu.VMEM((4, SUB, 128), f32),
            pltpu.VMEM((SUB, BLOCK), f32),
            pltpu.SemaphoreType.DMA,
            pltpu.SemaphoreType.DMA((LAST,)),
            pltpu.SemaphoreType.DMA((LAST + 4,)),
        ],
        compiler_params=pltpu.CompilerParams(
            has_side_effects=True, vmem_limit_bytes=50 * 1024 * 1024
        ),
    )(grouped, stats)
    return adjacency, connectivity[:, 0]


def solution(mesh):
    names = ("x", "zl", "y", "zh", "k")
    finer = Mesh(mesh.devices.reshape(4, 4, 4, 2, 2), names)
    cells, genes = names[:3], names[3:]
    return jax.shard_map(
        shards,
        mesh=finer,
        in_specs=(P(cells, genes), P(cells)),
        out_specs=(P(cells, genes), P(cells)),
        check_vma=False,
    )
```

time: 406 us -> 157 us (0.39)
  waiting for transfers between devices: 332 us -> 0 us
  Pallas kernels: 0 us -> 144 us
  blocking collectives: 22 us -> 0 us
  between operations: 13.8 us -> 0.66 us
  matrix products: 12 us -> 0 us
  starting transfers between devices: 9.05 us -> 0 us
    reduce_scatter x3 -> x0, waiting for transfers between devices: 214 us -> none  [sum_in_order(): blocks = lax.psum_scatter(blocks, axes[k], scatter_dimension=0, tiled=True)]
    pallas_call x0 -> x1, Pallas kernels: none -> 144 us  [shards(): pl.pallas_call(kernel, name='network', out_shape=(jax.ShapeDtypeStruct((S...]
    all_gather x1 -> x0, waiting for transfers between devices: 118 us -> none  [shards(): full_block = lax.all_gather(own_block, 'genes', axis=1, tiled=True)]
    all_to_all x1 -> x0, blocking collectives: 12.4 us -> none  [from_everyone(): return lax.all_to_all(copies, axis, split_axis=0, concat_axis=0, tiled=True)]
    dot_general x1 -> x0, matrix products: 12 us -> none  [cross_product(): lax.dot_general(left, right, (((0,), (0,)), ((), ())), preferred_element_...]
    all_gather x1 -> x0, blocking collectives: 9.55 us -> none  [turned_gather(): out, at, outs = (lax.all_gather(both, axis, axis=0, tiled=True), 0, [])]
    all_to_all x1 -> x0, starting transfers between devices: 8.89 us -> none  [from_everyone(): return lax.all_to_all(copies, axis, split_axis=0, concat_axis=0, tiled=True)]
    transpose x1 -> x0, local copies, waits for them, and re-layouts: 6.57 us -> none  [sum_in_order(): jnp.moveaxis(blocks, sequence, range(len(axes))).reshape(-1, *inside)]
  transfers between devices with their start and end apart: 5 -> 0, of which waited for: 4 -> 0; matrix products, arithmetic and copies ran while one was open for 0% -> 0% of each run, Pallas kernels for 0% -> 0%
where the time goes in v1:
time: 157 us; the launch traced here: 156 us
  Pallas kernels  144 us (92%)
  other arithmetic  6.3 us (4%)
  local copies, waits for them, and re-layouts  4.9 us (3%)
    pallas_call x1, Pallas kernels, shards(): pl.pallas_call(kernel, name='network', out_shape=(jax.ShapeDtypeStruct((S...  144 us
    reduce_sum x1, other arithmetic, shards(): halves = jnp.sum(wide, axis=1)  5.59 us
    reshape x2, local copies, waits for them, and re-layouts, shards(): grouped = own.reshape(BLOCK, 2, 2, QUARTER).transpose(2, 1, 0, 3)  3.57 us

profile of v1, /device:TPU:1, one launch (start us, length us, event | category | flops | bytes accessed | tf_op | source)
XLA Modules:
  0.0 156.1 jit_solution(8471196483984547620)
XLA Ops:
  0.6 0.7 convert_divide_fusion
  1.3 5.6 %convert_reduce_fusion = (f32[2,1024]{1,0:T(2,128)S(1)}, f32[2,1024]{1,0:T(2,128)S(1)}, bf16[1024,1024]{1,0:T(8,128)(2,1)}) fusion(f32[1024]{0:T(1024)S(1)} %convert_divide_fusion, s32[1024,1024]{1,0:T(8,128)} %param.2), kind=kLoop, calls=%fused_computation.1 | loop fusion | flops 7335936 | bytes 6311936 | tf_op jit(solution)/shard_map/reduce_sum | solution.py:421
  6.9 3.3 %reshape.17 = bf16[1024,2,2,256]{3,2,1,0:T(2,128)(2,1)S(1)} reshape(bf16[1024,1024]{1,0:T(8,128)(2,1)} %get-tuple-element.8) | data formatting | bytes 4194304 | tf_op jit(solution)/shard_map/reshape | solution.py:423
  10.2 0.3 copy.5
  10.5 144.2 %network.1 = (f32[64,1024]{1,0:T(8,128)S(1)}, f32[64,128]{1,0:T(8,128)S(1)}) custom-call(bf16[4,1024,256]{2,1,0:T(8,128)(2,1)S(1)} %bitcast.7, f32[4,1024]{1,0:T(4,128)S(1)} %pad_maximum_fusion.stat_ref), custom_call_target="tpu_custom_call" | custom-call | tf_op jit(solution)/shard_map/network/pallas_call | solution.py:429
  154.8 0.6 slice_reduce_fusion
  155.4 0.7 copy.7
  (1 shorter events, 0.0 us)

commit v2 on v1

v2 whole, which is shorter than its diff:
```python
import functools

import jax
import jax.numpy as jnp
from jax import lax
from jax.experimental import pallas as pl
from jax.experimental.pallas import tpu as pltpu
from jax.sharding import Mesh
from jax.sharding import PartitionSpec as P

MESH = pl.DeviceIdType.MESH
BLOCK = 1024
SUB = 64
QUARTER = 256
LEVELS = 8190.0
CELLS_ALL = 65536.0


def kernel(
    counts_ref, library_ref, adj_ref, conn_ref,
    raw, xa, xb, gr, gt, tt, f1, d1, r1, f2, d2, r2, zs, zr, ms, mr,
    st, sz, sx, sy, sc, sq, cm, cu, cw, rowv, cr, total_ref,
    load_sem, send_sem, recv_sem,
):
    x, zl, y = lax.axis_index("x"), lax.axis_index("zl"), lax.axis_index("y")
    zh, k = lax.axis_index("zh"), lax.axis_index("k")
    z = zh * 4 + zl
    spot = {"x": x, "y": y}
    mine = 2 * zh + k
    used = [0]
    started = []

    def remote(src, dst, where):
        n = used[0]
        used[0] += 1
        copy = pltpu.make_async_remote_copy(
            src_ref=src,
            dst_ref=dst,
            send_sem=send_sem.at[n],
            recv_sem=recv_sem.at[n],
            device_id=where,
            device_id_type=MESH,
        )
        copy.start()
        started.append(copy)
        return copy

    def along_z(hops):
        there = lax.rem(z + hops + 8, 8)
        return {"zh": there // 4, "zl": lax.rem(there, 4)}

    def hop(axis, by):
        return {axis: lax.rem(spot[axis] + by + 4, 4)}

    barrier = pltpu.get_barrier_semaphore()
    greeted = [along_z(d) for d in range(1, 8)] + [{"k": 1 - k}]
    greeted += [hop(axis, d) for axis in ("x", "y") for d in (1, 2, 3)]
    for where in greeted:
        pl.semaphore_signal(barrier, inc=1, device_id=where, device_id_type=MESH)

    halves = (1 - zh, zh)
    loads = []
    for n in range(4):
        rows = pl.ds(pl.multiple_of(halves[n // 2] * 512 + (n % 2) * 256, 256), 256)
        loads.append(
            (rows, pltpu.make_async_copy(counts_ref.at[rows], raw.at[rows], load_sem.at[n]))
        )
        loads[-1][1].start()
    factor = 10000.0 / library_ref[...].astype(jnp.float32)
    cw[...] = jnp.broadcast_to(factor, (128, BLOCK)).T
    for n in range(4):
        rows, load = loads[n]
        load.wait()
        if n % 2 == 0:
            sq[...] = jnp.zeros_like(sq)

        def piece(i, carry, n=n):
            at = pl.ds(
                pl.multiple_of(halves[n // 2] * 512 + (n % 2) * 256 + i * 64, 64), 64
            )
            scale = cw[at]
            scale = jnp.concatenate([scale, scale], axis=1)
            for g in range(4):
                hi, lo = g % 2, g // 2
                lanes = pl.ds((2 * hi + lo) * QUARTER, QUARTER)
                value = jnp.log1p(raw[at, lanes].astype(jnp.float32) * scale)
                value = value.astype(jnp.bfloat16)
                xa[k, g, at] = value
                value = value.astype(jnp.float32).reshape(8, 8, QUARTER)
                sq[0, :, lanes] = sq[0, :, lanes] + jnp.sum(value, axis=0)
                sq[1, :, lanes] = sq[1, :, lanes] + jnp.sum(value * value, axis=0)
            return carry

        lax.fori_loop(0, 4, piece, 0)
        if n % 2:
            st[pl.ds(halves[n // 2], 1)] = jnp.sum(sq[0], axis=0, keepdims=True)
            st[pl.ds(2 + halves[n // 2], 1)] = jnp.sum(sq[1], axis=0, keepdims=True)
    pl.semaphore_wait(barrier, len(greeted))

    sz[z] = st[...]
    stat_z = [remote(st, sz.at[z], along_z(d)) for d in (4, 3, 5, 2, 6, 1, 7)]
    partner_x = remote(xa.at[k], xa.at[k], {"k": 1 - k})
    far_half = pl.multiple_of((1 - zh) * 512, 512)
    arriving = [
        remote(xa.at[k, i, pl.ds(far_half, 512)], xb.at[k, i], along_z(4))
        for i in range(4)
    ]

    def to_partner(i):
        arriving[i].wait_recv()
        return remote(xb.at[k, i], xb.at[k, i], {"k": 1 - k})

    ones = jnp.ones((BLOCK, 128), jnp.bfloat16)

    def raw_gram(a, lo):
        def body(hi, carry):
            t = 2 * a + hi
            turned = xa[a, 2 * lo + hi].T
            gt[lo, t] = jnp.dot(turned, ones, preferred_element_type=jnp.float32)
            for q in range(4):
                gr[lo, t, :, q * QUARTER : (q + 1) * QUARTER] = jnp.dot(
                    turned,
                    xa[k, (q % 2) * 2 + q // 2],
                    preferred_element_type=jnp.float32,
                )
            return carry

        lax.fori_loop(0, 2, body, 0)

    raw_gram(k, 0)
    raw_gram(k, 1)

    for c in stat_z:
        c.wait_recv()

    def column(h):
        parts = [
            (sz[4 * h + i, b : b + 1], sz[4 * h + i, 2 + b : 3 + b])
            for i in range(4)
            for b in range(2)
        ]
        total = functools.reduce(jnp.add, [p[0] for p in parts])
        squares = functools.reduce(jnp.add, [p[1] for p in parts])
        mean = total * (1.0 / 4096.0)
        norms = [p[1] - 2.0 * mean * p[0] + 512.0 * mean * mean for p in parts]
        norm = functools.reduce(jnp.maximum, norms) * 1.0001 + squares * 2.5e-7 + 1e-2
        return total, squares, jnp.sqrt(norm)

    for h in range(2):
        for i, v in enumerate(column(h)):
            sx[x, 4 * h + i : 4 * h + i + 1] = v

    def spread(ref, axis):
        here = spot[axis]
        return [remote(ref.at[here], ref.at[here], hop(axis, d)) for d in (1, 3, 2)]

    def gathered(copies, ref, cells, out, slot):
        for c in copies:
            c.wait_recv()
        for h in range(2):
            parts = [
                [ref[i, 4 * h + r : 4 * h + r + 1] for r in range(3)] for i in range(4)
            ]
            total = parts[0][0] + parts[1][0] + parts[2][0] + parts[3][0]
            squares = parts[0][1] + parts[1][1] + parts[2][1] + parts[3][1]
            mean = total * (0.25 / cells)
            norms = [
                p[2] + (512.0**0.5) * jnp.abs(p[0] * (1.0 / cells) - mean) for p in parts
            ]
            norm = functools.reduce(jnp.maximum, norms)
            for i, v in enumerate((total, squares, norm)):
                out[slot, 4 * h + i : 4 * h + i + 1] = v

    copies = spread(sx, "x")
    partner_x.wait_recv()
    raw_gram(1 - k, 0)
    gathered(copies, sx, 4096.0, sy, y)
    copies = spread(sy, "y")
    raw_gram(1 - k, 1)
    gathered(copies, sy, 16384.0, sc, k)
    other_core = remote(sc.at[k], sc.at[k], {"k": 1 - k})
    other_core.wait_recv()
    for b in range(4):
        h, core = b // 2, b % 2
        rows = sc[core, 4 * h : 4 * h + 4]
        mean = rows[0:1] * (1.0 / CELLS_ALL)
        unit = (LEVELS / 2.0) ** 0.5 / rows[2:3]
        variance = rows[1:2] * (1.0 / CELLS_ALL) - mean * mean
        rowv[b, 0:1] = mean
        rowv[b, 1:2] = unit
        rowv[b, 2:3] = lax.rsqrt(variance + 1e-05) / unit

    def columns(side):
        for a in range(2):
            b = 2 * side + a
            cm[b] = jnp.broadcast_to(rowv[b, 0:1], (128, BLOCK)).T
            cu[b] = jnp.broadcast_to(rowv[b, 1:2], (128, BLOCK)).T

    columns(zh)
    own_mean, own_unit = rowv[mine, 0:1], rowv[mine, 1:2]
    for e, total in enumerate((st[0:1] + st[1:2], st[pl.ds(zh, 1)])):
        sq[e, 0:1] = own_mean * own_unit * (1.0 + e)
        sq[e, 1:2] = total * own_unit * (1.0 + e)
        sq[e, 2:3] = own_unit * (1.0 + e)

    wide = lambda v: jnp.concatenate([v, v], axis=1)

    def rounded(e, lo, q, a, hi, gram, factors):
        unit, off, mean = factors
        at = pl.ds(q * QUARTER, QUARTER)
        value = (
            gram * unit * sq[e, 2:3, at] - off * sq[e, 0:1, at] - mean * sq[e, 1:2, at]
        )
        value = jnp.clip(value, -LEVELS, LEVELS)
        code = jnp.round(value).astype(jnp.int32).astype(jnp.int16)
        rows = pl.ds(pl.multiple_of(hi * SUB, SUB), SUB)
        for c in range(2):
            part = code[:, c * 128 : (c + 1) * 128].reshape(4, SUB, 128)
            if q < 2:
                tt[2 * e + lo, q, 2 * a + c, :, rows] = part
            else:
                tt[2 * e + lo, q, :, pl.ds(2 * a + c, 1), rows] = part[:, None]

    def row_factors(e, lo, a, hi, total):
        side = lax.rem(zh + e, 2)
        first = pl.multiple_of((2 * hi + lo) * QUARTER, QUARTER)
        mean = cm[2 * side + a, pl.ds(first, QUARTER)]
        unit = cu[2 * side + a, pl.ds(first, QUARTER)]
        off = (total - (512.0 if e else 1024.0) * mean) * unit
        return wide(unit), wide(off), wide(mean * unit)

    def own_codes(lo, q):
        def body(t, carry):
            a, hi = t // 2, lax.rem(t, 2)
            factors = row_factors(0, lo, a, hi, gt[lo, t])
            gram = gr[lo, t, :, q * QUARTER : (q + 1) * QUARTER]
            rounded(0, lo, q, a, hi, gram, factors)
            return carry

        lax.fori_loop(0, 4, body, 0)

    def cross_codes(lo):
        def body(t, carry):
            a, hi = t // 2, lax.rem(t, 2)
            turned = xb[a, 2 * lo + hi].T
            total = jnp.dot(turned, ones[:512], preferred_element_type=jnp.float32)
            factors = row_factors(1, lo, a, hi, total)
            near = pl.ds(pl.multiple_of(zh * 512, 512), 512)
            for q in range(4):
                right = xa[k, (q % 2) * 2 + q // 2, near]
                gram = jnp.dot(turned, right, preferred_element_type=jnp.float32)
                rounded(1, lo, q, a, hi, gram, factors)
            return carry

        lax.fori_loop(0, 4, body, 0)

    axes = [("x", "y", -1), ("x", "y", 1), ("y", "x", -1), ("y", "x", 1)]

    def at4(axis, by):
        return lax.rem(spot[axis] + by + 4, 4)

    class Ring:
        def __init__(self, tile, axis, s, far, direct, relay):
            self.tile, self.axis, self.s = tile, axis, s
            self.far, self.direct, self.relay = far, direct, relay
            self.c_far = remote(tile(at4(axis, 2)), far, hop(axis, s))
            self.c_direct = remote(tile(at4(axis, -s)), direct, hop(axis, -s))

        def pass_on(self):
            self.c_far.wait_recv()
            here = self.tile(at4(self.axis, self.s))
            here[...] = here[...] + self.far[...]
            self.c_relay = remote(here, self.relay, hop(self.axis, self.s))

        def total(self):
            self.c_direct.wait_recv()
            self.c_relay.wait_recv()
            here = self.tile(spot[self.axis])
            return here[...] + self.direct[...] + self.relay[...]

    rings1, rings2 = {}, {}

    def p1(j, q):
        first, _, s = axes[q]
        rings1[j, q] = Ring(
            lambda d: tt.at[j, q, d], first, s, f1.at[j, q], d1.at[j, q], r1.at[j, q]
        )

    def p2(j):
        for q in range(4):
            rings1[j, q].pass_on()

    def p3(j):
        for q, (first, second, s) in enumerate(axes):
            total = rings1[j, q].total().astype(jnp.int32)
            here = spot[first]
            tt[j, q, here] = ((total + 2) >> 2).astype(jnp.int16)
            rings2[j, q] = Ring(
                lambda d, q=q, here=here: tt.at[j, q, here, d],
                second, s, f2.at[j, q], d2.at[j, q], r2.at[j, q],
            )

    def p4(j):
        for q in range(4):
            rings2[j, q].pass_on()

    last_sends = []

    def p5(j):
        e, lo = j // 2, j % 2
        for q in range(4):
            total = rings2[j, q].total()
            for hi in range(2):
                zs[j, hi, :, q * 128 : (q + 1) * 128] = total[hi * SUB : (hi + 1) * SUB]
        to_x = 2 * lax.rem(zh + e, 2) + x // 2
        c = lax.rem(x, 2)
        for hi in range(2):
            to_zl = 2 * hi + lo
            stays = jnp.logical_and(to_x == x, to_zl == zl)
            n = used[0]
            used[0] += 1
            copy = pltpu.make_async_remote_copy(
                src_ref=zs.at[j, hi],
                dst_ref=zr.at[c, zl],
                send_sem=send_sem.at[n],
                recv_sem=recv_sem.at[LAST + c * 4 + zl],
                device_id={"x": to_x, "zl": to_zl},
                device_id_type=MESH,
            )

            @pl.when(jnp.logical_not(stays))
            def _(copy=copy):
                copy.start()

            @pl.when(stays)
            def _(hi=hi):
                zr[c, zl] = zs[j, hi]

            last_sends.append((stays, copy))

    for lo in range(2):
        for q in range(4):
            own_codes(lo, q)
            p1(lo, q)
    columns(1 - zh)
    p2(0)
    p2(1)
    partner_b = [to_partner(0), to_partner(1)]
    p3(0)
    partner_b[0].wait_recv()
    partner_b[1].wait_recv()
    cross_codes(0)
    for q in range(4):
        p1(2, q)
    p3(1)
    p4(0)
    p4(1)
    p2(2)
    p5(0)
    p5(1)
    p3(2)
    cw[...] = jnp.broadcast_to(rowv[x, 2:3], (128, BLOCK)).T
    partner_b += [to_partner(2), to_partner(3)]
    partner_b[2].wait_recv()
    partner_b[3].wait_recv()
    cross_codes(1)
    for q in range(4):
        p1(3, q)
    p4(2)
    p2(3)
    p5(2)
    p3(3)
    p4(3)
    p5(3)

    for c in range(2):
        from_x = 2 * lax.rem(x, 2) + c
        for s in range(4):
            arrives = jnp.logical_not(jnp.logical_and(from_x == x, zl == s))

            @pl.when(arrives)
            def _(c=c, s=s, from_x=from_x):
                pltpu.make_async_remote_copy(
                    src_ref=zs.at[0, 0],
                    dst_ref=zr.at[c, s],
                    send_sem=send_sem.at[0],
                    recv_sem=recv_sem.at[LAST + c * 4 + s],
                    device_id={"x": from_x, "zl": s},
                    device_id_type=MESH,
                ).wait_recv()

    for q in range(4):
        for c in range(2):
            at = slice(q * 128, (q + 1) * 128)
            parts = [zr[c, s, :, at].astype(jnp.int32) for s in range(4)]
            first = q * QUARTER + c * 128
            total_ref[:, first : first + 128] = functools.reduce(jnp.add, parts).astype(
                jnp.float32
            )

    crossed = (x // 2) != zh
    mirror = []
    for dz in (2, 1, 3, 0):
        for dy in (2, 1, 3, 0):
            there_z, there_y = lax.rem(zl + dz, 4), lax.rem(y + dy, 4)
            n = used[0]
            used[0] += 1
            mirror.append(
                pltpu.make_async_remote_copy(
                    src_ref=ms.at[there_z * 4 + there_y],
                    dst_ref=mr.at[zl * 4 + y],
                    send_sem=send_sem.at[n],
                    recv_sem=recv_sem.at[n],
                    device_id={
                        "x": mine, "zl": there_z, "y": there_y,
                        "zh": x // 2, "k": lax.rem(x, 2),
                    },
                    device_id_type=MESH,
                )
            )

    @pl.when(crossed)
    def _():
        low = lax.broadcasted_iota(jnp.int32, (32, 128), 1) < SUB
        for m in range(8):
            part = jnp.round(total_ref[:, m * 128 : (m + 1) * 128] * 0.25)
            top, bottom = part[:32], part[32:]
            even = jnp.where(low, top, pltpu.roll(bottom, SUB, 1))
            odd = jnp.where(low, pltpu.roll(top, SUB, 1), bottom)
            ms[2 * m] = even.astype(jnp.int32).astype(jnp.int16)
            ms[2 * m + 1] = odd.astype(jnp.int32).astype(jnp.int16)
        for c in mirror:
            c.start()
        for c in mirror:
            c.wait_recv()
        for m in range(8):
            pieces = []
            for s in (2 * m, 2 * m + 1):
                part = mr[s].astype(jnp.int32).astype(jnp.float32)
                pieces += [part, pltpu.roll(part, SUB, 1)]
            turned = jnp.concatenate(pieces, axis=0).T[:SUB]
            at = slice(m * 128, (m + 1) * 128)
            total_ref[:, at] = total_ref[:, at] * 0.5 + 2.0 * turned
        for c in mirror:
            c.wait_send()

    first = pl.multiple_of((zl * 4 + y) * SUB, SUB)
    weight = cw[pl.ds(first, SUB)] * (4.0 / CELLS_ALL)
    row = x * BLOCK + first + lax.broadcasted_iota(jnp.int32, (SUB, 128), 0)
    partial = jnp.zeros((SUB, 128), jnp.float32)
    for m in range(8):
        at = pl.ds(m * 128, 128)
        value = total_ref[:, at] * weight * rowv[mine, 2:3, at]
        square = value * value
        power = square * square * square
        lane = mine * BLOCK + m * 128 + lax.broadcasted_iota(jnp.int32, (SUB, 128), 1)
        power = jnp.where(row == lane, 0.0, power)
        adj_ref[:, at] = power
        partial = partial + power
    both = jnp.concatenate([partial, jnp.zeros_like(partial)], axis=0).T
    cr[3] = jnp.broadcast_to(jnp.sum(both, axis=0, keepdims=True), (8, 128))
    to = [{"k": 1 - k}, {"zh": 1 - zh}, {"k": 1 - k, "zh": 1 - zh}]
    ends = [remote(cr.at[3], cr.at[i], where) for i, where in enumerate(to)]
    for c in ends:
        c.wait_recv()
    conn_ref[...] = cr[0] + cr[1] + cr[2] + cr[3]
    for c in started:
        c.wait_send()
    for stays, copy in last_sends:

        @pl.when(jnp.logical_not(stays))
        def _(copy=copy):
            copy.wait_send()

    assert used[0] <= LAST, used[0]


LAST = 170


def shards(counts, library):
    i16, f32, bf16 = jnp.int16, jnp.float32, jnp.bfloat16
    vmem = pl.BlockSpec(memory_space=pltpu.VMEM)
    wide_buffer = pltpu.VMEM((4, 4, 4, 128, 128), i16)
    small_buffer = pltpu.VMEM((4, 4, 128, 128), i16)
    adjacency, connectivity = pl.pallas_call(
        kernel,
        name="network",
        out_shape=(
            jax.ShapeDtypeStruct((SUB, BLOCK), f32),
            jax.ShapeDtypeStruct((8, 128), f32),
        ),
        in_specs=[pl.BlockSpec(memory_space=pl.ANY), vmem],
        out_specs=(vmem, vmem),
        scratch_shapes=[
            pltpu.VMEM((BLOCK, BLOCK), jnp.int32),
            pltpu.VMEM((2, 4, BLOCK, QUARTER), bf16),
            pltpu.VMEM((2, 4, 512, QUARTER), bf16),
            pltpu.VMEM((2, 4, QUARTER, BLOCK), f32),
            pltpu.VMEM((2, 4, QUARTER, 128), f32),
            pltpu.VMEM((4, 4, 4, 4, 128, 128), i16),
            wide_buffer, wide_buffer, wide_buffer,
            small_buffer, small_buffer, small_buffer,
            pltpu.VMEM((4, 2, SUB, 512), i16),
            pltpu.VMEM((2, 4, SUB, 512), i16),
            pltpu.VMEM((16, 32, 128), i16),
            pltpu.VMEM((16, 32, 128), i16),
            pltpu.VMEM((4, BLOCK), f32),
            pltpu.VMEM((8, 4, BLOCK), f32),
            pltpu.VMEM((4, 8, BLOCK), f32),
            pltpu.VMEM((4, 8, BLOCK), f32),
            pltpu.VMEM((2, 8, BLOCK), f32),
            pltpu.VMEM((2, 8, BLOCK), f32),
            pltpu.VMEM((4, BLOCK, 128), f32),
            pltpu.VMEM((4, BLOCK, 128), f32),
            pltpu.VMEM((BLOCK, 128), f32),
            pltpu.VMEM((4, 8, BLOCK), f32),
            pltpu.VMEM((4, 8, 128), f32),
            pltpu.VMEM((SUB, BLOCK), f32),
            pltpu.SemaphoreType.DMA((4,)),
            pltpu.SemaphoreType.DMA((LAST,)),
            pltpu.SemaphoreType.DMA((LAST + 8,)),
        ],
        compiler_params=pltpu.CompilerParams(
            collective_id=0, has_side_effects=True, vmem_limit_bytes=56 * 1024 * 1024
        ),
    )(counts, library.reshape(1, BLOCK))
    return adjacency, connectivity[0, :SUB]


def solution(mesh):
    names = ("x", "zl", "y", "zh", "k")
    finer = Mesh(mesh.devices.reshape(4, 4, 4, 2, 2), names)
    cells, genes = names[:3], names[3:]
    return jax.shard_map(
        shards,
        mesh=finer,
        in_specs=(P(cells, genes), P(cells)),
        out_specs=(P(cells, genes), P(cells)),
        check_vma=False,
    )
```

time: 157 us -> 134 us (0.85)
  Pallas kernels: 144 us -> 130 us
  other arithmetic: 6.3 us -> 0 us
  local copies, waits for them, and re-layouts: 4.9 us -> 2.87 us
    pallas_call x1, Pallas kernels: 144 us -> 130 us  [shards(): pl.pallas_call(kernel, name='network', out_shape=(jax.ShapeDtypeStruct((S...]
    reduce_sum x1 -> x0, other arithmetic: 5.59 us -> none  [shards(): halves = jnp.sum(wide, axis=1)]
    reshape x2 -> x0, local copies, waits for them, and re-layouts: 3.57 us -> none  [shards(): grouped = own.reshape(BLOCK, 2, 2, QUARTER).transpose(2, 1, 0, 3)]
where the time goes in v2:
time: 134 us
  Pallas kernels  130 us (97%)
  local copies, waits for them, and re-layouts  2.87 us (2%)
    pallas_call x1, Pallas kernels, shards(): pl.pallas_call(kernel, name='network', out_shape=(jax.ShapeDtypeStruct((S...  130 us

profile of v2, /device:TPU:1, one launch (start us, length us, event | category | flops | bytes accessed | tf_op | source)
XLA Modules:
  0.0 133.9 jit_solution(483769175314348749)
XLA Ops:
  0.6 130.4 %network.1 = (f32[64,1024]{1,0:T(8,128)}, f32[8,128]{1,0:T(8,128)}) custom-call(s32[1024,1024]{1,0:T(8,128)} %counts_ref.1, s32[1,1024]{1,0:T(1,128)} %bitcast.3), custom_call_target="tpu_custom_call" | custom-call | tf_op jit(solution)/shard_map/network/pallas_call | solution.py:486
  131.1 1.2 slice_bitcast_fusion
  132.3 1.7 %copy.5 = f32[64,1024]{1,0:T(8,128)} copy(f32[64,1024]{1,0:T(8,128)} %get-tuple-element.8) | data formatting | bytes 524288

commit v3 on v2

--- a/solution.py
+++ b/solution.py
@@ -18,7 +18,7 @@
 
 def kernel(
     counts_ref, library_ref, adj_ref, conn_ref,
-    raw, xa, xb, gr, gt, tt, f1, d1, r1, f2, d2, r2, zs, zr, ms, mr,
+    raw, xa, xb, rl, gr, gt, tt, f1, d1, r1, f2, d2, r2, zs, zr, xs, xr, ms, mr,
     st, sz, sx, sy, sc, sq, cm, cu, cw, rowv, cr, total_ref,
     load_sem, send_sem, recv_sem,
 ):
@@ -53,7 +53,9 @@
         return {axis: lax.rem(spot[axis] + by + 4, 4)}
 
     barrier = pltpu.get_barrier_semaphore()
-    greeted = [along_z(d) for d in range(1, 8)] + [{"k": 1 - k}]
+    half_z = [{"zl": lax.rem(zl + d, 4)} for d in (3, 1, 2)]
+    greeted = half_z + [{"k": 1 - k}, {"zh": 1 - zh}, {"zh": 1 - zh, "k": 1 - k}]
+    greeted += [along_z(2), along_z(-2)]
     greeted += [hop(axis, d) for axis in ("x", "y") for d in (1, 2, 3)]
     for where in greeted:
         pl.semaphore_signal(barrier, inc=1, device_id=where, device_id_type=MESH)
@@ -97,17 +99,38 @@
             st[pl.ds(2 + halves[n // 2], 1)] = jnp.sum(sq[1], axis=0, keepdims=True)
     pl.semaphore_wait(barrier, len(greeted))
 
-    sz[z] = st[...]
-    stat_z = [remote(st, sz.at[z], along_z(d)) for d in (4, 3, 5, 2, 6, 1, 7)]
+    sz[zl] = st[...]
+    stat_z = [remote(st, sz.at[zl], where) for where in half_z]
     partner_x = remote(xa.at[k], xa.at[k], {"k": 1 - k})
     far_half = pl.multiple_of((1 - zh) * 512, 512)
-    arriving = [
-        remote(xa.at[k, i, pl.ds(far_half, 512)], xb.at[k, i], along_z(4))
-        for i in range(4)
-    ]
+
+    ways = (along_z(2), along_z(-2))
+    leg_one, leg_two = {}, {}
+
+    def send_genes(i):
+        leg_one[i] = [
+            remote(
+                xa.at[k, i, pl.ds(pl.multiple_of(far_half + 256 * f, 256), 256)],
+                rl.at[f, i],
+                ways[f],
+            )
+            for f in range(2)
+        ]
+
+    def forward(i):
+        for c in leg_one[i]:
+            c.wait_recv()
+        leg_two[i] = [
+            remote(rl.at[f, i], xb.at[k, i, pl.ds(256 * f, 256)], ways[f])
+            for f in range(2)
+        ]
+
+    send_genes(0)
+    send_genes(1)
 
     def to_partner(i):
-        arriving[i].wait_recv()
+        for c in leg_two[i]:
+            c.wait_recv()
         return remote(xb.at[k, i], xb.at[k, i], {"k": 1 - k})
 
     ones = jnp.ones((BLOCK, 128), jnp.bfloat16)
@@ -133,22 +156,14 @@
     for c in stat_z:
         c.wait_recv()
 
-    def column(h):
-        parts = [
-            (sz[4 * h + i, b : b + 1], sz[4 * h + i, 2 + b : 3 + b])
-            for i in range(4)
-            for b in range(2)
-        ]
-        total = functools.reduce(jnp.add, [p[0] for p in parts])
-        squares = functools.reduce(jnp.add, [p[1] for p in parts])
-        mean = total * (1.0 / 4096.0)
-        norms = [p[1] - 2.0 * mean * p[0] + 512.0 * mean * mean for p in parts]
-        norm = functools.reduce(jnp.maximum, norms) * 1.0001 + squares * 2.5e-7 + 1e-2
-        return total, squares, jnp.sqrt(norm)
-
-    for h in range(2):
-        for i, v in enumerate(column(h)):
-            sx[x, 4 * h + i : 4 * h + i + 1] = v
+    parts = [(sz[i, b : b + 1], sz[i, 2 + b : 3 + b]) for i in range(4) for b in range(2)]
+    total = functools.reduce(jnp.add, [p[0] for p in parts])
+    squares = functools.reduce(jnp.add, [p[1] for p in parts])
+    mean = total * (1.0 / 4096.0)
+    norms = [p[1] - 2.0 * mean * p[0] + 512.0 * mean * mean for p in parts]
+    norm = functools.reduce(jnp.maximum, norms) * 1.0001 + squares * 2.5e-7 + 1e-2
+    for i, v in enumerate((total, squares, jnp.sqrt(norm))):
+        sx[x, i : i + 1] = v
 
     def spread(ref, axis):
         here = spot[axis]
@@ -157,45 +172,47 @@
     def gathered(copies, ref, cells, out, slot):
         for c in copies:
             c.wait_recv()
-        for h in range(2):
-            parts = [
-                [ref[i, 4 * h + r : 4 * h + r + 1] for r in range(3)] for i in range(4)
-            ]
-            total = parts[0][0] + parts[1][0] + parts[2][0] + parts[3][0]
-            squares = parts[0][1] + parts[1][1] + parts[2][1] + parts[3][1]
-            mean = total * (0.25 / cells)
-            norms = [
-                p[2] + (512.0**0.5) * jnp.abs(p[0] * (1.0 / cells) - mean) for p in parts
-            ]
-            norm = functools.reduce(jnp.maximum, norms)
-            for i, v in enumerate((total, squares, norm)):
-                out[slot, 4 * h + i : 4 * h + i + 1] = v
+        parts = [[ref[i, r : r + 1] for r in range(3)] for i in range(4)]
+        total = parts[0][0] + parts[1][0] + parts[2][0] + parts[3][0]
+        squares = parts[0][1] + parts[1][1] + parts[2][1] + parts[3][1]
+        mean = total * (0.25 / cells)
+        norms = [
+            p[2] + (512.0**0.5) * jnp.abs(p[0] * (1.0 / cells) - mean) for p in parts
+        ]
+        norm = functools.reduce(jnp.maximum, norms)
+        for i, v in enumerate((total, squares, norm)):
+            out[slot, i : i + 1] = v
 
     copies = spread(sx, "x")
     partner_x.wait_recv()
+    forward(0)
     raw_gram(1 - k, 0)
     gathered(copies, sx, 4096.0, sy, y)
     copies = spread(sy, "y")
     raw_gram(1 - k, 1)
-    gathered(copies, sy, 16384.0, sc, k)
-    other_core = remote(sc.at[k], sc.at[k], {"k": 1 - k})
-    other_core.wait_recv()
-    for b in range(4):
-        h, core = b // 2, b % 2
-        rows = sc[core, 4 * h : 4 * h + 4]
-        mean = rows[0:1] * (1.0 / CELLS_ALL)
-        unit = (LEVELS / 2.0) ** 0.5 / rows[2:3]
-        variance = rows[1:2] * (1.0 / CELLS_ALL) - mean * mean
-        rowv[b, 0:1] = mean
-        rowv[b, 1:2] = unit
-        rowv[b, 2:3] = lax.rsqrt(variance + 1e-05) / unit
+    gathered(copies, sy, 16384.0, sc, mine)
+    stat_core = remote(sc.at[mine], sc.at[mine], {"k": 1 - k})
+    stat_far = [
+        remote(sc.at[mine], sc.at[mine], {"zh": 1 - zh}),
+        remote(sc.at[mine], sc.at[mine], {"zh": 1 - zh, "k": 1 - k}),
+    ]
+    forward(1)
+    send_genes(2)
+    send_genes(3)
 
     def columns(side):
         for a in range(2):
             b = 2 * side + a
-            cm[b] = jnp.broadcast_to(rowv[b, 0:1], (128, BLOCK)).T
-            cu[b] = jnp.broadcast_to(rowv[b, 1:2], (128, BLOCK)).T
-
+            mean = sc[b, 0:1] * (1.0 / CELLS_ALL)
+            unit = (LEVELS / 2.0) ** 0.5 / sc[b, 2:3]
+            variance = sc[b, 1:2] * (1.0 / CELLS_ALL) - mean * mean
+            rowv[b, 0:1] = mean
+            rowv[b, 1:2] = unit
+            rowv[b, 2:3] = lax.rsqrt(variance + 1e-05) / unit
+            cm[b] = jnp.broadcast_to(mean, (128, BLOCK)).T
+            cu[b] = jnp.broadcast_to(unit, (128, BLOCK)).T
+
+    stat_core.wait_recv()
     columns(zh)
     own_mean, own_unit = rowv[mine, 0:1], rowv[mine, 1:2]
     for e, total in enumerate((st[0:1] + st[1:2], st[pl.ds(zh, 1)])):
@@ -264,7 +281,12 @@
             self.tile, self.axis, self.s = tile, axis, s
             self.far, self.direct, self.relay = far, direct, relay
             self.c_far = remote(tile(at4(axis, 2)), far, hop(axis, s))
-            self.c_direct = remote(tile(at4(axis, -s)), direct, hop(axis, -s))
+
+        def send_direct(self):
+            s = self.s
+            self.c_direct = remote(
+                self.tile(at4(self.axis, -s)), self.direct, hop(self.axis, -s)
+            )
 
         def pass_on(self):
             self.c_far.wait_recv()
@@ -299,6 +321,8 @@
                 lambda d, q=q, here=here: tt.at[j, q, here, d],
                 second, s, f2.at[j, q], d2.at[j, q], r2.at[j, q],
             )
+        for q in range(4):
+            rings2[j, q].send_direct()
 
     def p4(j):
         for q in range(4):
@@ -312,127 +336,148 @@
             total = rings2[j, q].total()
             for hi in range(2):
                 zs[j, hi, :, q * 128 : (q + 1) * 128] = total[hi * SUB : (hi + 1) * SUB]
+        for hi in range(2):
+            hand_over(zs.at[j, hi], zr.at[e, zl], {"zl": 2 * hi + lo}, 2 * hi + lo == zl, e * 4 + zl)
+
+    def hand_over(src, dst, where, stays, slot):
+        n = used[0]
+        used[0] += 1
+        copy = pltpu.make_async_remote_copy(
+            src_ref=src,
+            dst_ref=dst,
+            send_sem=send_sem.at[n],
+            recv_sem=recv_sem.at[LAST + slot],
+            device_id=where,
+            device_id_type=MESH,
+        )
+
+        @pl.when(jnp.logical_not(stays))
+        def _():
+            copy.start()
+
+        @pl.when(stays)
+        def _():
+            dst[...] = src[...]
+
+        last_sends.append((stays, copy))
+
+    def arrival(src, dst, slot):
+        return pltpu.make_async_remote_copy(
+            src_ref=src,
+            dst_ref=dst,
+            send_sem=send_sem.at[0],
+            recv_sem=recv_sem.at[LAST + slot],
+            device_id={"k": 1 - k},
+            device_id_type=MESH,
+        )
+
+    c_here = lax.rem(x, 2)
+
+    def settle(e):
+        for s in range(4):
+
+            @pl.when(zl != s)
+            def _(s=s):
+                arrival(zs.at[0, 0], zr.at[e, s], e * 4 + s).wait_recv()
+
+        for q in range(4):
+            at = slice(q * 128, (q + 1) * 128)
+            parts = [zr[e, s, :, at].astype(jnp.int32) for s in range(4)]
+            code = (functools.reduce(jnp.add, parts) + 2) >> 2
+            xs[e, :, at] = code.astype(jnp.int16)
+            if e:
+                low = lax.broadcasted_iota(jnp.int32, (32, 128), 1) < SUB
+                part = code.astype(jnp.float32)
+                top, bottom = part[:32], part[32:]
+                even = jnp.where(low, top, pltpu.roll(bottom, SUB, 1))
+                odd = jnp.where(low, pltpu.roll(top, SUB, 1), bottom)
+                for half, v in enumerate((even, odd)):
+                    ms[2 * q + half] = v.astype(jnp.int32).astype(jnp.int16)
+        if e:
+            for n in range(8):
+                slot = used[0]
+                used[0] += 1
+                copy = pltpu.make_async_remote_copy(
+                    src_ref=ms.at[n],
+                    dst_ref=mr.at[zl * 4 + y],
+                    send_sem=send_sem.at[slot],
+                    recv_sem=recv_sem.at[LAST + 10 + zl * 4 + y],
+                    device_id={
+                        "x": mine, "zl": n // 2, "y": 2 * c_here + n % 2,
+                        "zh": 1 - zh, "k": x // 2,
+                    },
+                    device_id_type=MESH,
+                )
+                copy.start()
+                started.append(copy)
         to_x = 2 * lax.rem(zh + e, 2) + x // 2
-        c = lax.rem(x, 2)
-        for hi in range(2):
-            to_zl = 2 * hi + lo
-            stays = jnp.logical_and(to_x == x, to_zl == zl)
-            n = used[0]
-            used[0] += 1
-            copy = pltpu.make_async_remote_copy(
-                src_ref=zs.at[j, hi],
-                dst_ref=zr.at[c, zl],
-                send_sem=send_sem.at[n],
-                recv_sem=recv_sem.at[LAST + c * 4 + zl],
-                device_id={"x": to_x, "zl": to_zl},
-                device_id_type=MESH,
-            )
-
-            @pl.when(jnp.logical_not(stays))
-            def _(copy=copy):
-                copy.start()
-
-            @pl.when(stays)
-            def _(hi=hi):
-                zr[c, zl] = zs[j, hi]
-
-            last_sends.append((stays, copy))
+        hand_over(xs.at[e], xr.at[c_here], {"x": to_x}, to_x == x, 8 + c_here)
+
+    def directs(j):
+        for q in range(4):
+            rings1[j, q].send_direct()
 
     for lo in range(2):
         for q in range(4):
             own_codes(lo, q)
             p1(lo, q)
+        directs(lo)
+    p2(0)
+    partner_b = [to_partner(0), to_partner(1)]
+    for c in stat_far:
+        c.wait_recv()
     columns(1 - zh)
-    p2(0)
     p2(1)
-    partner_b = [to_partner(0), to_partner(1)]
-    p3(0)
+    forward(2)
     partner_b[0].wait_recv()
     partner_b[1].wait_recv()
     cross_codes(0)
     for q in range(4):
         p1(2, q)
+    directs(2)
+    p3(0)
+    forward(3)
+    cw[...] = jnp.broadcast_to(rowv[x, 2:3], (128, BLOCK)).T
     p3(1)
     p4(0)
+    p2(2)
     p4(1)
-    p2(2)
+    partner_b += [to_partner(2)]
     p5(0)
+    partner_b += [to_partner(3)]
     p5(1)
-    p3(2)
-    cw[...] = jnp.broadcast_to(rowv[x, 2:3], (128, BLOCK)).T
-    partner_b += [to_partner(2), to_partner(3)]
     partner_b[2].wait_recv()
     partner_b[3].wait_recv()
     cross_codes(1)
     for q in range(4):
         p1(3, q)
+    directs(3)
+    p3(2)
+    settle(0)
+    p2(3)
     p4(2)
-    p2(3)
+    p3(3)
     p5(2)
-    p3(3)
     p4(3)
     p5(3)
 
+    settle(1)
+
     for c in range(2):
-        from_x = 2 * lax.rem(x, 2) + c
-        for s in range(4):
-            arrives = jnp.logical_not(jnp.logical_and(from_x == x, zl == s))
-
-            @pl.when(arrives)
-            def _(c=c, s=s, from_x=from_x):
-                pltpu.make_async_remote_copy(
-                    src_ref=zs.at[0, 0],
-                    dst_ref=zr.at[c, s],
-                    send_sem=send_sem.at[0],
-                    recv_sem=recv_sem.at[LAST + c * 4 + s],
-                    device_id={"x": from_x, "zl": s},
-                    device_id_type=MESH,
-                ).wait_recv()
-
-    for q in range(4):
-        for c in range(2):
-            at = slice(q * 128, (q + 1) * 128)
-            parts = [zr[c, s, :, at].astype(jnp.int32) for s in range(4)]
+
+        @pl.when(2 * lax.rem(x, 2) + c != x)
+        def _(c=c):
+            arrival(xs.at[0], xr.at[c], 8 + c).wait_recv()
+
+        for q in range(4):
             first = q * QUARTER + c * 128
-            total_ref[:, first : first + 128] = functools.reduce(jnp.add, parts).astype(
-                jnp.float32
-            )
-
-    crossed = (x // 2) != zh
-    mirror = []
-    for dz in (2, 1, 3, 0):
-        for dy in (2, 1, 3, 0):
-            there_z, there_y = lax.rem(zl + dz, 4), lax.rem(y + dy, 4)
-            n = used[0]
-            used[0] += 1
-            mirror.append(
-                pltpu.make_async_remote_copy(
-                    src_ref=ms.at[there_z * 4 + there_y],
-                    dst_ref=mr.at[zl * 4 + y],
-                    send_sem=send_sem.at[n],
-                    recv_sem=recv_sem.at[n],
-                    device_id={
-                        "x": mine, "zl": there_z, "y": there_y,
-                        "zh": x // 2, "k": lax.rem(x, 2),
-                    },
-                    device_id_type=MESH,
-                )
-            )
-
-    @pl.when(crossed)
+            part = xr[c, :, q * 128 : (q + 1) * 128].astype(jnp.int32)
+            total_ref[:, first : first + 128] = 4.0 * part.astype(jnp.float32)
+
+    @pl.when((x // 2) != zh)
     def _():
-        low = lax.broadcasted_iota(jnp.int32, (32, 128), 1) < SUB
-        for m in range(8):
-            part = jnp.round(total_ref[:, m * 128 : (m + 1) * 128] * 0.25)
-            top, bottom = part[:32], part[32:]
-            even = jnp.where(low, top, pltpu.roll(bottom, SUB, 1))
-            odd = jnp.where(low, pltpu.roll(top, SUB, 1), bottom)
-            ms[2 * m] = even.astype(jnp.int32).astype(jnp.int16)
-            ms[2 * m + 1] = odd.astype(jnp.int32).astype(jnp.int16)
-        for c in mirror:
-            c.start()
-        for c in mirror:
-            c.wait_recv()
+        for s in range(16):
+            arrival(ms.at[0], mr.at[s], 10 + s).wait_recv()
         for m in range(8):
             pieces = []
             for s in (2 * m, 2 * m + 1):
@@ -441,8 +486,6 @@
             turned = jnp.concatenate(pieces, axis=0).T[:SUB]
             at = slice(m * 128, (m + 1) * 128)
             total_ref[:, at] = total_ref[:, at] * 0.5 + 2.0 * turned
-        for c in mirror:
-            c.wait_send()
 
     first = pl.multiple_of((zl * 4 + y) * SUB, SUB)
     weight = cw[pl.ds(first, SUB)] * (4.0 / CELLS_ALL)
@@ -475,7 +518,7 @@
     assert used[0] <= LAST, used[0]
 
 
-LAST = 170
+LAST = 190
 
 
 def shards(counts, library):
@@ -496,6 +539,7 @@
             pltpu.VMEM((BLOCK, BLOCK), jnp.int32),
             pltpu.VMEM((2, 4, BLOCK, QUARTER), bf16),
             pltpu.VMEM((2, 4, 512, QUARTER), bf16),
+            pltpu.VMEM((2, 4, QUARTER, QUARTER), bf16),
             pltpu.VMEM((2, 4, QUARTER, BLOCK), f32),
             pltpu.VMEM((2, 4, QUARTER, 128), f32),
             pltpu.VMEM((4, 4, 4, 4, 128, 128), i16),
@@ -503,13 +547,15 @@
             small_buffer, small_buffer, small_buffer,
             pltpu.VMEM((4, 2, SUB, 512), i16),
             pltpu.VMEM((2, 4, SUB, 512), i16),
-            pltpu.VMEM((16, 32, 128), i16),
+            pltpu.VMEM((2, SUB, 512), i16),
+            pltpu.VMEM((2, SUB, 512), i16),
+            pltpu.VMEM((8, 32, 128), i16),
             pltpu.VMEM((16, 32, 128), i16),
             pltpu.VMEM((4, BLOCK), f32),
-            pltpu.VMEM((8, 4, BLOCK), f32),
-            pltpu.VMEM((4, 8, BLOCK), f32),
-            pltpu.VMEM((4, 8, BLOCK), f32),
-            pltpu.VMEM((2, 8, BLOCK), f32),
+            pltpu.VMEM((4, 4, BLOCK), f32),
+            pltpu.VMEM((4, 4, BLOCK), f32),
+            pltpu.VMEM((4, 4, BLOCK), f32),
+            pltpu.VMEM((4, 4, BLOCK), f32),
             pltpu.VMEM((2, 8, BLOCK), f32),
             pltpu.VMEM((4, BLOCK, 128), f32),
             pltpu.VMEM((4, BLOCK, 128), f32),
@@ -519,7 +565,7 @@
             pltpu.VMEM((SUB, BLOCK), f32),
             pltpu.SemaphoreType.DMA((4,)),
             pltpu.SemaphoreType.DMA((LAST,)),
-            pltpu.SemaphoreType.DMA((LAST + 8,)),
+            pltpu.SemaphoreType.DMA((LAST + 26,)),
         ],
         compiler_params=pltpu.CompilerParams(
             collective_id=0, has_side_effects=True, vmem_limit_bytes=56 * 1024 * 1024

time: 134 us -> 115 us (0.86)
  Pallas kernels: 130 us -> 111 us
    pallas_call x1, Pallas kernels: 130 us -> 111 us  [shards(): pl.pallas_call(kernel, name='network', out_shape=(jax.ShapeDtypeStruct((S...]
where the time goes in v3:
time: 115 us; the launch traced here: 114 us
  Pallas kernels  111 us (97%)
  local copies, waits for them, and re-layouts  2.87 us (2%)
    pallas_call x1, Pallas kernels, shards(): pl.pallas_call(kernel, name='network', out_shape=(jax.ShapeDtypeStruct((S...  111 us

profile of v3, /device:TPU:1, one launch (start us, length us, event | category | flops | bytes accessed | tf_op | source)
XLA Modules:
  0.0 114.4 jit_solution(14459290988019582367)
XLA Ops:
  0.6 110.9 %network.1 = (f32[64,1024]{1,0:T(8,128)}, f32[8,128]{1,0:T(8,128)}) custom-call(s32[1024,1024]{1,0:T(8,128)} %counts_ref.1, s32[1,1024]{1,0:T(1,128)} %bitcast.3), custom_call_target="tpu_custom_call" | custom-call | tf_op jit(solution)/shard_map/network/pallas_call | solution.py:529
  111.5 1.2 %slice_bitcast_fusion = f32[64]{0:T(128)} fusion(f32[8,128]{1,0:T(8,128)} %get-tuple-element.5), kind=kLoop, calls=%fused_computation | loop fusion | bytes 512 | tf_op jit(solution)/shard_map/squeeze | solution.py:574
  112.7 1.7 %copy.5 = f32[64,1024]{1,0:T(8,128)} copy(f32[64,1024]{1,0:T(8,128)} %get-tuple-element.8) | data formatting | bytes 524288

commit v4 on v3

--- a/solution.py
+++ b/solution.py
@@ -439,13 +439,10 @@
     forward(3)
     cw[...] = jnp.broadcast_to(rowv[x, 2:3], (128, BLOCK)).T
     p3(1)
+    p2(2)
     p4(0)
-    p2(2)
     p4(1)
-    partner_b += [to_partner(2)]
-    p5(0)
-    partner_b += [to_partner(3)]
-    p5(1)
+    partner_b += [to_partner(2), to_partner(3)]
     partner_b[2].wait_recv()
     partner_b[3].wait_recv()
     cross_codes(1)
@@ -453,12 +450,14 @@
         p1(3, q)
     directs(3)
     p3(2)
-    settle(0)
+    p5(0)
+    p5(1)
     p2(3)
     p4(2)
     p3(3)
     p5(2)
     p4(3)
+    settle(0)
     p5(3)
 
     settle(1)
@@ -506,7 +505,7 @@
     ends = [remote(cr.at[3], cr.at[i], where) for i, where in enumerate(to)]
     for c in ends:
         c.wait_recv()
-    conn_ref[...] = cr[0] + cr[1] + cr[2] + cr[3]
+    conn_ref[...] = (cr[0] + cr[1] + cr[2] + cr[3])[0:1, :SUB]
     for c in started:
         c.wait_send()
     for stays, copy in last_sends:
@@ -531,7 +530,7 @@
         name="network",
         out_shape=(
             jax.ShapeDtypeStruct((SUB, BLOCK), f32),
-            jax.ShapeDtypeStruct((8, 128), f32),
+            jax.ShapeDtypeStruct((1, SUB), f32),
         ),
         in_specs=[pl.BlockSpec(memory_space=pl.ANY), vmem],
         out_specs=(vmem, vmem),
@@ -571,7 +570,7 @@
             collective_id=0, has_side_effects=True, vmem_limit_bytes=56 * 1024 * 1024
         ),
     )(counts, library.reshape(1, BLOCK))
-    return adjacency, connectivity[0, :SUB]
+    return adjacency, connectivity.reshape(SUB)
 
 
 def solution(mesh):

time: 115 us -> 111 us (0.965)
  Pallas kernels: 111 us -> 107 us
    pallas_call x1, Pallas kernels: 111 us -> 107 us  [shards(): pl.pallas_call(kernel, name='network', out_shape=(jax.ShapeDtypeStruct((S...]
    squeeze x1 -> x0, local copies, waits for them, and re-layouts: 1.2 us -> none  [shards(): return (adjacency, connectivity[0, :SUB])]
    unnamed x1 -> x2, local copies, waits for them, and re-layouts: 1.67 us -> 2.8 us
where the time goes in v4:
time: 111 us
  Pallas kernels  107 us (96%)
  local copies, waits for them, and re-layouts  2.8 us (3%)
    pallas_call x1, Pallas kernels, shards(): pl.pallas_call(kernel, name='network', out_shape=(jax.ShapeDtypeStruct((S...  107 us
    unnamed x2, local copies, waits for them, and re-layouts  2.8 us

profile of v4, /device:TPU:1, one launch (start us, length us, event | category | flops | bytes accessed | tf_op | source)
XLA Modules:
  0.0 110.6 jit_solution(3283300292037264064)
XLA Ops:
  0.6 107.1 %network.1 = (f32[64,1024]{1,0:T(8,128)}, f32[1,64]{1,0:T(1,128)}) custom-call(s32[1024,1024]{1,0:T(8,128)} %counts_ref.1, s32[1,1024]{1,0:T(1,128)} %bitcast.2), custom_call_target="tpu_custom_call" | custom-call | tf_op jit(solution)/shard_map/network/pallas_call | solution.py:528
  107.7 1.7 %copy.6 = f32[64,1024]{1,0:T(8,128)} copy(f32[64,1024]{1,0:T(8,128)} %get-tuple-element.8) | data formatting | bytes 524288
  109.4 1.1 %copy.7 = f32[64]{0:T(128)} copy(f32[64]{0:T(128)} %bitcast.3) | data formatting | bytes 512

commit v5 on v4

--- a/solution.py
+++ b/solution.py
@@ -532,7 +532,7 @@
             jax.ShapeDtypeStruct((SUB, BLOCK), f32),
             jax.ShapeDtypeStruct((1, SUB), f32),
         ),
-        in_specs=[pl.BlockSpec(memory_space=pl.ANY), vmem],
+        in_specs=[pl.BlockSpec(memory_space=pltpu.HBM), vmem],
         out_specs=(vmem, vmem),
         scratch_shapes=[
             pltpu.VMEM((BLOCK, BLOCK), jnp.int32),
@@ -567,7 +567,7 @@
             pltpu.SemaphoreType.DMA((LAST + 26,)),
         ],
         compiler_params=pltpu.CompilerParams(
-            collective_id=0, has_side_effects=True, vmem_limit_bytes=56 * 1024 * 1024
+            collective_id=0, has_side_effects=True, vmem_limit_bytes=48 * 1024 * 1024
         ),
     )(counts, library.reshape(1, BLOCK))
     return adjacency, connectivity.reshape(SUB)

time: 111 us -> 110 us (level)
  local copies, waits for them, and re-layouts: 2.8 us -> 4.08 us
    pallas_call x1, Pallas kernels: 107 us -> 106 us  [shards(): pl.pallas_call(kernel, name='network', out_shape=(jax.ShapeDtypeStruct((S...]
    unnamed x2 -> x6, local copies, waits for them, and re-layouts: 2.8 us -> 4.08 us
where the time goes in v5:
time: 110 us
  Pallas kernels  106 us (96%)
  local copies, waits for them, and re-layouts  4.08 us (4%)
    pallas_call x1, Pallas kernels, shards(): pl.pallas_call(kernel, name='network', out_shape=(jax.ShapeDtypeStruct((S...  106 us
    unnamed x6, local copies, waits for them, and re-layouts  4.08 us

profile of v5, /device:TPU:1, one launch (start us, length us, event | category | flops | bytes accessed | tf_op | source)
XLA Modules:
  0.0 110.3 jit_solution(4951241259560578043)
XLA Ops:
  0.6 0.0 copy-start
  0.6 2.2 %copy-done = s32[1024,1024]{1,0:T(8,128)S(1)} copy-done((s32[1024,1024]{1,0:T(8,128)S(1)}, s32[1024,1024]{1,0:T(8,128)}, u32[]{:S(2)}) %copy-start) | copy-done | bytes 4194328
  2.8 0.0 copy-start.1
  2.8 0.7 copy-done.1
  3.5 105.6 %network.1 = (f32[64,1024]{1,0:T(8,128)S(1)}, f32[1,64]{1,0:T(1,128)S(1)}) custom-call(s32[1024,1024]{1,0:T(8,128)S(1)} %copy-done, s32[1,1024]{1,0:T(1,128)S(1)} %bitcast.2), custom_call_target="tpu_custom_call" | custom-call | tf_op jit(solution)/shard_map/network/pallas_call | solution.py:528
  109.1 0.7 copy.6
  109.8 0.5 copy.7
Async XLA Ops:
  0.6 2.2 %copy-start = (s32[1024,1024]{1,0:T(8,128)S(1)}, s32[1024,1024]{1,0:T(8,128)}, u32[]{:S(2)}) copy-start(s32[1024,1024]{1,0:T(8,128)} %counts_ref.1) | copy-start | bytes 12582916
  2.8 0.7 copy-start.1
